TPU v7x, 32 devices: a whole 2x2x4 slice. The times are simulated.
32 devices in a mesh: dp: 8 (over y, x, core), tensor: 4 (over z).
Axes of the slice: x: 2, y: 2, z: 4, core: 2. Of those that a mesh axis runs over, the one named last changes fastest.
Arguments:
- activations: bfloat16 [1, 1024, 4096], P(None, ('dp', 'tensor')), may hold values from -6 to 6
- out_grad: bfloat16 [1, 1024, 512], P(None, 'dp', 'tensor'), may hold values from -0.5 to 0.5
- value_weight: bfloat16 [1, 512, 4096], P(None, 'tensor'), may hold values from -6 to 6
- error_feedback: bfloat16 [1, 8, 512, 4096], P(None, 'dp', 'tensor'), may hold values from -8 to 8
- warm_right: bfloat16 [1, 4, 4096, 32], P(None, 'tensor'), may hold values from -6 to 6
Outputs:
- new_error: bfloat16 [1, 8, 512, 4096], P(None, 'dp', 'tensor')
- left_basis: float32 [1, 512, 32], P(None, 'tensor')
- right_factor: bfloat16 [1, 4, 4096, 32], P(None, 'tensor')
- input_grad: bfloat16 [1, 1024, 4096], P(None, ('dp', 'tensor'))
All inputs are finite; a program needn't handle non-finite values.
Results may differ from a plain program's by a relative error of at most 0.00065.
Values may be sent and summed in bfloat16 or wider, within the bound.
A program may use at most 64 MiB of HBM per device.

v0:
```python
import functools

import jax
import jax.numpy as jnp
from jax import lax
from jax.experimental import pallas as pl
from jax.experimental.pallas import tpu as pltpu
from jax.sharding import PartitionSpec as P

MESH = pl.DeviceIdType.MESH
F32 = jnp.float32
BF16 = jnp.bfloat16
CHUNKS = 4


def split(x):
    high = x.astype(BF16)
    return high, (x - high.astype(F32)).astype(BF16)


def dot(a, b):
    return jnp.dot(a, b, preferred_element_type=F32)


def dot_nt(a, b):
    return lax.dot_general(a, b, (((1,), (1,)), ((), ())), preferred_element_type=F32)


def orthonormal(left, halfway):
    rank = left.shape[0]
    gram = lax.dot_general(
        left, left, (((1,), (1,)), ((), ())), precision=lax.Precision.HIGHEST, preferred_element_type=F32
    )
    row = lax.broadcasted_iota(jnp.int32, (rank, 1), 0)
    for k in range(rank):
        if k == rank // 2:
            halfway()
        scale = lax.rsqrt(gram[k : k + 1, k : k + 1])
        gram_row = gram[k : k + 1, :] * scale
        left_row = left[k : k + 1, :] * scale
        column = jnp.where(row > k, gram[:, k : k + 1] * scale, 0.0)
        gram = gram - column * gram_row
        left = jnp.where(row == k, left_row, left - column * left_row)
    return left


def kernel(
    ndp, nt, act_hbm, og_hbm, weight_hbm, error_hbm, warm_hbm,
    residual, basis_out, factor, input_grad,
    og, error, warm, loads, grad_sum, tokens, wall, oall, merged, lefts, part, halves, parts, right,
    act_send, act_recv, w_send, w_recv, f_send, f_recv, d_send, d_recv,
    o_send, o_recv, l_send, l_recv, h_send, h_recv, p_send, p_recv, r_send, r_recv, t_send,
):
    dp = lax.axis_index("dp")
    me = lax.axis_index("tensor")
    rows, width = act_hbm.shape
    head = og.shape[1]
    rank = warm.shape[0]
    spread = min(ndp, 8)
    slice_rows = head // spread
    cw = width // CHUNKS

    def copy(src, dst, send, recv, **device):
        return pltpu.make_async_remote_copy(
            src_ref=src, dst_ref=dst, send_sem=send, recv_sem=recv, device_id=device, device_id_type=MESH
        )

    def z_peer(o):
        return lax.rem(me + o, nt)

    def dp_peer(o):
        return lax.rem(dp + o, ndp)

    own_rows = pl.ds(pl.multiple_of(me * rows, rows), rows)
    loading = [
        pltpu.make_async_copy(src, dst, loads.at[i])
        for i, (src, dst) in enumerate((
            (act_hbm, tokens.at[own_rows, :]), (og_hbm, og), (weight_hbm, wall.at[me]),
            (error_hbm, error), (warm_hbm, warm),
        ))
    ]
    for load in loading:
        load.start()

    barrier = pltpu.get_barrier_semaphore()
    for o in range(1, nt):
        pl.semaphore_signal(barrier, inc=1, device_id={"tensor": z_peer(o)}, device_id_type=MESH)
    for o in range(1, ndp):
        pl.semaphore_signal(barrier, inc=1, device_id={"dp": dp_peer(o)}, device_id_type=MESH)
    pl.semaphore_wait(barrier, nt + ndp - 2)

    def token_block(b, c):
        return tokens.at[pl.ds(pl.multiple_of(b * rows, rows), rows), pl.ds(c * cw, cw)]

    own_slice = lax.rem(dp, spread)

    def weight_rows(s):
        return pl.ds(pl.multiple_of(s * slice_rows, slice_rows), slice_rows)

    def token_copy(b, c, way):
        return copy(
            token_block(b, c), token_block(b, c), act_send.at[way, b, c], act_recv.at[b, c],
            tensor=jnp.clip(me + (1 - 2 * way), 0, nt - 1),
        )

    def weight_copy(b, way):
        place = wall.at[b, weight_rows(own_slice), :]
        return copy(
            place, place, w_send.at[way, b], w_recv.at[b],
            tensor=jnp.clip(me + (1 - 2 * way), 0, nt - 1),
        )

    def has_next(way):
        return me < nt - 1 if way == 0 else me > 0

    def origin(way, s):
        b = me - s if way == 0 else me + s
        return b, (b >= 0 if way == 0 else b < nt), jnp.clip(b, 0, nt - 1)

    loading[0].wait()
    for c in range(CHUNKS):
        for way in range(2):
            @pl.when(has_next(way))
            def _():
                token_copy(me, c, way).start()
    loading[1].wait()
    for o in range(1, nt):
        q = z_peer(o)
        copy(
            og.at[pl.ds(pl.multiple_of(q * rows, rows), rows), :], oall.at[me], o_send.at[q], o_recv.at[me], tensor=q
        ).start()

    oall[me] = og[own_rows, :]
    og_t = og[...].astype(F32).T.astype(BF16)

    group = dp - own_slice
    core = lax.rem(dp, 2)
    chip = dp // 2
    partner = dp + 1 - 2 * core
    chips = spread // 2

    def slice_copy(b, s, q, send, recv):
        return copy(wall.at[b, weight_rows(s), :], wall.at[b, weight_rows(s), :], send, recv, dp=q)

    def chip_slice(o):
        return 2 * lax.rem(own_slice // 2 + o, chips) + core

    def chip_copy(b, o):
        s = chip_slice(o)
        return slice_copy(b, own_slice, group + s, f_send.at[b, s], f_recv.at[b, own_slice])

    def partner_copy(b, o):
        s = chip_slice(o)
        return slice_copy(b, s, partner, d_send.at[b, s], d_recv.at[b, s])

    def weight_relay(s):
        for way in range(2):
            _, valid, b = origin(way, s)

            @pl.when(valid)
            def _():
                weight_copy(b, way).wait_recv()

            @pl.when(jnp.logical_and(valid, has_next(way)))
            def _():
                weight_copy(b, way).start()

            @pl.when(valid)
            def _():
                for o in range(1, chips):
                    chip_copy(b, o).start()
                partner_copy(b, 0).start()

    def weight_partner(s):
        for way in range(2):
            _, valid, b = origin(way, s)

            @pl.when(valid)
            def _():
                for o in range(1, chips):
                    q = chip_slice(o)
                    slice_copy(b, q, group + q, f_send.at[b, q], f_recv.at[b, q]).wait_recv()
                    partner_copy(b, o).start()

    def add_input(b, first=False):
        for c in range(CHUNKS):
            cols = slice(c * cw, (c + 1) * cw)
            term = dot(oall[b], wall[b, :, cols])
            grad_sum[:, cols] = term if first else grad_sum[:, cols] + term

    def input_part(s):
        for way in range(2):
            _, valid, b = origin(way, s)

            @pl.when(valid)
            def _():
                copy(oall.at[b], oall.at[b], o_send.at[b], o_recv.at[b], tensor=b).wait_recv()
                for o in range(chips):
                    q = chip_slice(o) + 1 - 2 * core
                    slice_copy(b, q, partner, d_send.at[b, q], d_recv.at[b, q]).wait_recv()
                add_input(b)

    for load in loading[2:]:
        load.wait()
    add_input(me, True)

    left = jnp.zeros((rank, head), F32)
    for s in range(1, nt):
        for c in range(CHUNKS):
            for way in range(2):
                _, valid, b = origin(way, s)

                @pl.when(valid)
                def _():
                    token_copy(b, c, way).wait_recv()

                @pl.when(jnp.logical_and(valid, has_next(way)))
                def _():
                    token_copy(b, c, way).start()
            if s == nt - 1:
                cols = slice(c * cw, (c + 1) * cw)
                m = dot(og_t, tokens[:, cols]) + error[:, cols].astype(F32)
                merged[:, cols] = m
                high, low = split(m)
                w = warm[:, cols]
                left += dot_nt(w, high) + dot_nt(w, low)
        if s == 1:
            for way in range(2):
                @pl.when(has_next(way))
                def _():
                    weight_copy(me, way).start()
        elif s < nt - 1:
            weight_relay(s - 1)

    lefts[dp] = left
    for o in range(1, ndp):
        q = dp_peer(o)
        copy(lefts.at[dp], lefts.at[dp], l_send.at[q], l_recv.at[dp], dp=q).start()
    if nt > 2:
        weight_relay(nt - 2)

    for o in range(1, ndp):
        q = dp_peer(o)
        copy(lefts.at[q], lefts.at[q], l_send.at[q], l_recv.at[q], dp=q).wait_recv()
    total = lefts[0]
    for q in range(1, ndp):
        total += lefts[q]
    basis_t = orthonormal(total * (1.0 / ndp), lambda: weight_relay(nt - 1))
    basis = basis_t.T
    basis_out[...] = basis_t
    bt_high, bt_low = split(basis_t)
    bt_both = jnp.concatenate([bt_high, bt_low], axis=0)

    nchip = ndp // 2
    ncol = min(ndp, width // 128)
    nrow = ndp // ncol
    pw, ph = width // ncol, rank // nrow

    def piece(q_chip, q_core):
        p = q_core * nchip + q_chip
        r, c = p // ncol, lax.rem(p, ncol)
        return (
            pl.ds(pl.multiple_of(r * ph, ph), ph) if nrow > 1 else pl.ds(0, ph),
            pl.ds(pl.multiple_of(c * pw, pw), pw),
        )

    def chip_peer(o):
        return lax.rem(chip + o, nchip)

    def half_copy(i):
        return copy(part.at[piece(i, 1 - core)], halves.at[i], h_send.at[i], h_recv.at[i], dp=partner)

    def part_copy(q, slot):
        return copy(part.at[piece(q, core)], parts.at[slot], p_send.at[q], p_recv.at[slot], dp=2 * q + core)

    def compute_part(c):
        cols = pl.ds(pl.multiple_of(c * pw, pw), pw)
        high, low = split(merged[:, cols])
        both = dot(bt_both, high)
        part[:, cols] = both[:rank] + both[rank:] + dot(bt_high, low)

    if nrow == 1:
        for o in range(nchip):
            i = chip_peer(o + 1)
            compute_part((1 - core) * nchip + i)
            half_copy(i).start()
        for i in range(nchip):
            compute_part(core * nchip + i)
    else:
        for c in range(ncol):
            compute_part(c)
        for o in range(nchip):
            half_copy(chip_peer(o + 1)).start()
    for o in range(1, nchip):
        q = chip_peer(o)
        half_copy(q).wait_recv()
        part[piece(q, core)] += halves[q]
        part_copy(q, chip).start()
    for s in range(1, nt - 1):
        weight_partner(s)
    half_copy(chip).wait_recv()
    mine = part[piece(chip, core)] + halves[chip]
    for o in range(1, nchip):
        q = chip_peer(o)
        part_copy(q, q).wait_recv()
        mine += parts[q]
    right[piece(chip, core)] = mine * (1.0 / ndp)

    def right_copy(q_chip, q_core, target, send):
        place = right.at[piece(q_chip, q_core)]
        return copy(place, place, send, r_recv.at[2 * q_chip + q_core], dp=target)

    for o in range(1, nchip):
        q = chip_peer(o)
        right_copy(chip, core, 2 * q + core, r_send.at[q]).start()
    right_copy(chip, core, partner, t_send.at[chip]).start()
    weight_partner(nt - 1)

    b_high, b_low = split(basis)
    b_cat = jnp.concatenate([b_high, b_low, b_high], axis=1)

    def finish(cols):
        r = right[:, cols]
        high, low = split(r)
        approx = dot(b_cat, jnp.concatenate([high, high, low], axis=0))
        residual[:, cols] = (merged[:, cols] - approx).astype(BF16)
        factor[:, cols] = high

    if nrow == 1:
        finish(piece(chip, core)[1])

    for s in range(1, nt - 2):
        input_part(s)
    for o in range(1, nchip):
        q = chip_peer(o)
        right_copy(q, core, partner, r_send.at[q]).wait_recv()
        right_copy(q, core, partner, t_send.at[q]).start()
        if nrow == 1:
            finish(piece(q, core)[1])
    if nt > 2:
        input_part(nt - 2)
    for o in range(nchip):
        q = chip_peer(o)
        right_copy(q, 1 - core, partner, r_send.at[q]).wait_recv()
        if nrow == 1:
            finish(piece(q, 1 - core)[1])
    if nrow > 1:
        for c in range(ncol):
            finish(pl.ds(c * pw, pw))

    input_part(nt - 1)
    input_grad[...] = grad_sum[...].astype(BF16)

    for way in range(2):
        @pl.when(has_next(way))
        def _():
            for c in range(CHUNKS):
                token_copy(me, c, way).wait_send()
            weight_copy(me, way).wait_send()
        for s in range(1, nt):
            _, valid, b = origin(way, s)

            @pl.when(jnp.logical_and(valid, has_next(way)))
            def _():
                for c in range(CHUNKS):
                    token_copy(b, c, way).wait_send()
                weight_copy(b, way).wait_send()
    for z in range(1, nt):
        b = z_peer(z)
        copy(oall.at[b], oall.at[b], o_send.at[b], o_recv.at[b], tensor=b).wait_send()
        for o in range(chips):
            s = chip_slice(o)
            if o:
                chip_copy(b, o).wait_send()
            partner_copy(b, o).wait_send()
    for o in range(1, ndp):
        q = dp_peer(o)
        copy(lefts.at[dp], lefts.at[dp], l_send.at[q], l_recv.at[dp], dp=q).wait_send()
    for o in range(nchip):
        q = chip_peer(o)
        half_copy(q).wait_send()
        right_copy(q, core, partner, t_send.at[q]).wait_send()
        if o:
            part_copy(q, chip).wait_send()
            right_copy(chip, core, 2 * q + core, r_send.at[q]).wait_send()


def local(activations, out_grad, value_weight, error_feedback, warm_right):
    ndp, nt = lax.axis_size("dp"), lax.axis_size("tensor")
    layers = [[], [], [], []]
    for layer in range(activations.shape[0]):
        outs = one_layer(
            ndp, nt, activations[layer], out_grad[layer], value_weight[layer],
            error_feedback[layer, 0], warm_right[layer, 0].T,
        )
        for kept, out in zip(layers, outs):
            kept.append(out)
    residual, basis, factor, input_grad = [jnp.stack(kept) for kept in layers]
    return residual[:, None], basis.swapaxes(1, 2), factor.swapaxes(1, 2)[:, None], input_grad


def one_layer(ndp, nt, act, og, weight, error, warm):
    rows, width = act.shape
    tok, head = og.shape
    rank = warm.shape[0]
    spread = min(ndp, 8)
    ncol = min(ndp, width // 128)
    nrow = ndp // ncol
    dma = pltpu.SemaphoreType.DMA
    vmem = pl.BlockSpec(memory_space=pltpu.VMEM)
    return pl.pallas_call(
        functools.partial(kernel, ndp, nt),
        out_shape=(
            jax.ShapeDtypeStruct((head, width), BF16),
            jax.ShapeDtypeStruct((rank, head), F32),
            jax.ShapeDtypeStruct((rank, width), BF16),
            jax.ShapeDtypeStruct((rows, width), BF16),
        ),
        in_specs=[pl.BlockSpec(memory_space=pltpu.HBM)] * 5,
        out_specs=(vmem,) * 4,
        scratch_shapes=[
            pltpu.VMEM((tok, head), BF16),
            pltpu.VMEM((head, width), BF16),
            pltpu.VMEM((rank, width), BF16),
            dma((5,)),
            pltpu.VMEM((rows, width), F32),
            pltpu.VMEM((tok, width), BF16),
            pltpu.VMEM((nt, head, width), BF16),
            pltpu.VMEM((nt, rows, head), BF16),
            pltpu.VMEM((head, width), F32),
            pltpu.VMEM((ndp, rank, head), F32),
            pltpu.VMEM((rank, width), F32),
            pltpu.VMEM((ndp // 2, rank // nrow, width // ncol), F32),
            pltpu.VMEM((ndp // 2, rank // nrow, width // ncol), F32),
            pltpu.VMEM((rank, width), F32),
            dma((2, nt, CHUNKS)), dma((nt, CHUNKS)),
            dma((2, nt)), dma((nt,)),
            dma((nt, spread)), dma((nt, spread)),
            dma((nt, spread)), dma((nt, spread)),
            dma((nt,)), dma((nt,)),
            dma((ndp,)), dma((ndp,)),
            dma((ndp // 2,)), dma((ndp // 2,)),
            dma((ndp // 2,)), dma((ndp // 2,)),
            dma((ndp // 2,)), dma((ndp,)), dma((ndp // 2,)),
        ],
        compiler_params=pltpu.CompilerParams(
            collective_id=0, has_side_effects=True, vmem_limit_bytes=63 * 1024 * 1024
        ),
    )(act, og, weight, error, warm)


def solution(mesh):
    return jax.shard_map(
        local,
        mesh=mesh,
        in_specs=(
            P(None, ("dp", "tensor"), None),
            P(None, "dp", "tensor"),
            P(None, "tensor", None),
            P(None, "dp", "tensor", None),
            P(None, "tensor", None, None),
        ),
        out_specs=(
            P(None, "dp", "tensor", None),
            P(None, "tensor", None),
            P(None, "tensor", None, None),
            P(None, ("dp", "tensor"), None),
        ),
        check_vma=False,
    )
```

profile of v0, /device:TPU:0, one launch (start us, length us, event | category | flops | bytes accessed | tf_op | source)
XLA Modules:
  0.0 60.8 jit_solution(12274283718042727308)
XLA Ops:
  0.6 55.5 %shard_map.84 = (bf16[128,4096]{1,0:T(8,128)(2,1)}, f32[32,128]{1,0:T(8,128)}, bf16[32,4096]{1,0:T(8,128)(2,1)}, bf16[32,4096]{1,0:T(8,128)(2,1)}) custom-call(bf16[32,4096]{1,0:T(8,128)(2,1)} %bitcast.22, bf16[128,128]{1,0:T(8,128)(2,1)} %bitcast.24, bf16[128,4096]{1,0:T(8,128)(2,1)} %bitcast.18, bf16[128,4096]{1,0:T(8,128)(2,1)} %bitcast.19, ...), custom_call_target="tpu_custom_call" | custom-call | tf_op jit(solution)/shard_map/pallas_call | solution.py:411
  56.1 0.0 copy-start.2
  56.1 0.0 copy-start.1
  56.1 2.3 %copy.13 = bf16[1,1,128,4096]{3,2,1,0:T(8,128)(2,1)} copy(bf16[1,1,128,4096]{3,2,1,0:T(8,128)(2,1)} %bitcast.17) | data formatting | bytes 2097152
  58.5 0.0 copy-done.2
  58.5 0.6 copy.14
  59.1 0.0 copy-done.1
  59.1 0.0 copy-start
  59.1 0.7 %copy.15 = bf16[1,1,4096,32]{2,3,1,0:T(8,128)(2,1)} copy(bf16[1,1,4096,32]{2,3,1,0:T(8,128)(2,1)S(1)} %bitcast.21) | data formatting | bytes 524288
  59.8 0.3 copy-done
  60.1 0.7 %copy.16 = bf16[1,32,4096]{2,1,0:T(8,128)(2,1)} copy(bf16[1,32,4096]{2,1,0:T(8,128)(2,1)S(1)} %bitcast.20) | data formatting | bytes 524288
Async XLA Ops:
  56.1 2.4 %copy-start.2 = (f32[32,128]{1,0:T(8,128)S(1)}, f32[32,128]{1,0:T(8,128)}, u32[]{:S(2)}) copy-start(f32[32,128]{1,0:T(8,128)} %get-tuple-element.9) | copy-start | bytes 49156
  56.1 3.0 %copy-start.1 = (bf16[32,4096]{1,0:T(8,128)(2,1)S(1)}, bf16[32,4096]{1,0:T(8,128)(2,1)}, u32[]{:S(2)}) copy-start(bf16[32,4096]{1,0:T(8,128)(2,1)} %get-tuple-element.10) | copy-start | bytes 786436
  59.1 1.0 %copy-start = (bf16[32,4096]{1,0:T(8,128)(2,1)S(1)}, bf16[32,4096]{1,0:T(8,128)(2,1)}, u32[]{:S(2)}) copy-start(bf16[32,4096]{1,0:T(8,128)(2,1)} %get-tuple-element.11) | copy-start | bytes 786436
where the time goes:
time: 61 us; the launch traced here: 60.8 us
  Pallas kernels  55.5 us (91%)
  local copies, waits for them, and re-layouts  4.69 us (8%)
  between operations  0.66 us (1%)
    pallas_call x1, Pallas kernels, one_layer(): pl.pallas_call(functools.partial(kernel, ndp, nt), out_shape=(jax.ShapeDt...  55.5 us
    unnamed x10, local copies, waits for them, and re-layouts  4.69 us

commit v1 on v0

--- a/solution.py
+++ b/solution.py
@@ -11,6 +11,7 @@
 F32 = jnp.float32
 BF16 = jnp.bfloat16
 CHUNKS = 4
+PIECES = 4
 
 
 def split(x):
@@ -385,6 +386,22 @@
             right_copy(chip, core, 2 * q + core, r_send.at[q]).wait_send()
 
 
+def write_out(*refs):
+    sems = refs[8]
+    copies = []
+    for i in range(4):
+        src, dst = refs[i], refs[4 + i]
+        count = PIECES if i == 0 else 2
+        step = src.shape[0] // count
+        for j in range(count):
+            rows = pl.ds(j * step, step)
+            copies.append(pltpu.make_async_copy(src.at[rows], dst.at[rows], sems.at[i, j]))
+    for c in copies:
+        c.start()
+    for c in copies:
+        c.wait()
+
+
 def local(activations, out_grad, value_weight, error_feedback, warm_right):
     ndp, nt = lax.axis_size("dp"), lax.axis_size("tensor")
     layers = [[], [], [], []]
@@ -408,14 +425,10 @@
     nrow = ndp // ncol
     dma = pltpu.SemaphoreType.DMA
     vmem = pl.BlockSpec(memory_space=pltpu.VMEM)
-    return pl.pallas_call(
+    shapes = (((head, width), BF16), ((rank, head), F32), ((rank, width), BF16), ((rows, width), BF16))
+    results = pl.pallas_call(
         functools.partial(kernel, ndp, nt),
-        out_shape=(
-            jax.ShapeDtypeStruct((head, width), BF16),
-            jax.ShapeDtypeStruct((rank, head), F32),
-            jax.ShapeDtypeStruct((rank, width), BF16),
-            jax.ShapeDtypeStruct((rows, width), BF16),
-        ),
+        out_shape=tuple(pltpu.VMEM(shape, dtype) for shape, dtype in shapes),
         in_specs=[pl.BlockSpec(memory_space=pltpu.HBM)] * 5,
         out_specs=(vmem,) * 4,
         scratch_shapes=[
@@ -444,9 +457,17 @@
             dma((ndp // 2,)), dma((ndp,)), dma((ndp // 2,)),
         ],
         compiler_params=pltpu.CompilerParams(
-            collective_id=0, has_side_effects=True, vmem_limit_bytes=63 * 1024 * 1024
+            collective_id=0, has_side_effects=True, vmem_limit_bytes=62 * 1024 * 1024
         ),
     )(act, og, weight, error, warm)
+    return pl.pallas_call(
+        write_out,
+        out_shape=tuple(jax.ShapeDtypeStruct(shape, dtype) for shape, dtype in shapes),
+        in_specs=[vmem] * 4,
+        out_specs=(pl.BlockSpec(memory_space=pltpu.HBM),) * 4,
+        scratch_shapes=[dma((4, PIECES))],
+        compiler_params=pltpu.CompilerParams(vmem_limit_bytes=16 * 1024 * 1024),
+    )(*results)
 
 
 def solution(mesh):

time: 61 us -> 56.4 us (0.925)
  local copies, waits for them, and re-layouts: 4.69 us -> 0 us
    unnamed x10 -> x0, local copies, waits for them, and re-layouts: 4.69 us -> none
    pallas_call x1 -> x2, Pallas kernels: 55.5 us -> 55.6 us  [the longest x1 54.3 us: one_layer(): pl.pallas_call(functools.partial(kernel, ndp, nt), out_shape=tuple((pltpu...]
where the time goes in v1:
time: 56.4 us; the launch traced here: 56.2 us
  Pallas kernels  55.6 us (99%)
  between operations  0.64 us (1%)
    pallas_call x1, Pallas kernels, one_layer(): pl.pallas_call(functools.partial(kernel, ndp, nt), out_shape=tuple((pltpu...  54.3 us
    pallas_call x1, Pallas kernels, one_layer(): pl.pallas_call(write_out, out_shape=tuple((jax.ShapeDtypeStruct(shape, dt...  1.28 us

profile of v1, /device:TPU:0, one launch (start us, length us, event | category | flops | bytes accessed | tf_op | source)
XLA Modules:
  0.0 56.2 jit_solution(15627916772265507676)
XLA Ops:
  0.6 54.3 %shard_map.84 = (bf16[128,4096]{1,0:T(8,128)(2,1)S(1)}, f32[32,128]{1,0:T(8,128)S(1)}, bf16[32,4096]{1,0:T(8,128)(2,1)S(1)}, bf16[32,4096]{1,0:T(8,128)(2,1)S(1)}) custom-call(bf16[32,4096]{1,0:T(8,128)(2,1)} %bitcast.19, bf16[128,128]{1,0:T(8,128)(2,1)} %bitcast.21, bf16[128,4096]{1,0:T(8,128)(2,1)} %bitcast.17, bf16[128,4096]{1,0:T(8,128)(2,1)} %bitcast.18, ...), custom_call_target="tpu_custom_call" | custom-call | tf_op jit(solution)/shard_map/pallas_call | solution.py:429
  55.0 1.3 %shard_map.85 = (bf16[128,4096]{1,0:T(8,128)(2,1)}, f32[32,128]{1,0:T(8,128)}, bf16[32,4096]{1,0:T(8,128)(2,1)}, bf16[32,4096]{1,0:T(8,128)(2,1)}) custom-call(bf16[128,4096]{1,0:T(8,128)(2,1)S(1)} %get-tuple-element.12.refs_0_, f32[32,128]{1,0:T(8,128)S(1)} %get-tuple-element.13.refs_1_, bf16[32,4096]{1,0:T(8,128)(2,1)S(1)} %get-tuple-element.14.refs_2_, ...), custom_call_target="tpu_custom_call" | custom-call | tf_op jit(solution)/shard_map/pallas_call | solution.py:463

commit v2 on v1

v2 whole, which is shorter than its diff:
```python
import functools

import jax
import jax.numpy as jnp
from jax import lax
from jax.experimental import pallas as pl
from jax.experimental.pallas import tpu as pltpu
from jax.sharding import PartitionSpec as P

MESH = pl.DeviceIdType.MESH
F32 = jnp.float32
BF16 = jnp.bfloat16
CHUNKS = 4
PIECES = 4
SUBS = 2


def split3(x):
    high = x.astype(BF16)
    rest = x - high.astype(F32)
    mid = rest.astype(BF16)
    return high, mid, (rest - mid.astype(F32)).astype(BF16)


def dot(a, b):
    return jnp.dot(a, b, preferred_element_type=F32)


def dot_nt(a, b):
    return lax.dot_general(a, b, (((1,), (1,)), ((), ())), preferred_element_type=F32)


def fold3(x):
    n = x.shape[0] // 3
    return x[:n] + x[n : 2 * n] + x[2 * n :]


def orthonormal(left):
    rank = left.shape[0]
    gram = lax.dot_general(
        left, left, (((1,), (1,)), ((), ())), precision=lax.Precision.HIGHEST, preferred_element_type=F32
    )
    row = lax.broadcasted_iota(jnp.int32, (rank, 1), 0)
    square = lax.broadcasted_iota(jnp.int32, (rank, rank), 0) == lax.broadcasted_iota(jnp.int32, (rank, rank), 1)
    gram = jnp.concatenate([gram, square.astype(F32)], axis=1)
    for k in range(rank):
        scale = lax.rsqrt(gram[k : k + 1, k : k + 1])
        gram_row = gram[k : k + 1, :] * scale
        left_row = left[k : k + 1, :] * scale
        column = jnp.where(row > k, gram[:, k : k + 1] * scale, 0.0)
        gram = jnp.where(row == k, gram_row, gram - column * gram_row)
        left = jnp.where(row == k, left_row, left - column * left_row)
    return left, gram[:, rank:]


def kernel(
    ndp, nt, act_hbm, og_hbm, weight_hbm, error_hbm, warm_hbm,
    residual, basis_out, factor, input_grad,
    og, stack, warm, wall, ogp, igs, merged, lefts, part, halves, parts, right,
    loads, act_send, act_recv, o_send, o_recv, g_send, g_recv, w_send, w_recv, i_send, i_recv,
    l_send, l_recv, h_send, h_recv, p_send, p_recv, r_send, r_recv, t_send, t_recv,
):
    dp = lax.axis_index("dp")
    me = lax.axis_index("tensor")
    rows, width = act_hbm.shape
    tok, head = og.shape
    rank = warm.shape[0]
    spread = ogp.shape[0]
    cw = width // CHUNKS
    wc = width // spread
    slot = lax.rem(dp, spread)
    group = dp - slot

    def copy(src, dst, send, recv, **device):
        return pltpu.make_async_remote_copy(
            src_ref=src, dst_ref=dst, send_sem=send, recv_sem=recv, device_id=device, device_id_type=MESH
        )

    def z_peer(o):
        return lax.rem(me + o, nt)

    def dp_peer(o):
        return lax.rem(dp + o, ndp)

    def group_peer(o):
        return lax.rem(slot + o, spread)

    def token_rows(b):
        return pl.ds(pl.multiple_of(b * rows, rows), rows)

    def slot_cols(s):
        return pl.ds(pl.multiple_of(s * wc, wc), wc)

    loading = [
        pltpu.make_async_copy(src, dst, loads.at[i])
        for i, (src, dst) in enumerate((
            (og_hbm, og), (act_hbm, stack.at[token_rows(me), :]), (og_hbm.at[token_rows(me), :], ogp.at[slot, me]),
            (warm_hbm, warm), (error_hbm, stack.at[pl.ds(tok, head), :]), (weight_hbm.at[:, slot_cols(slot)], wall.at[me]),
        ))
    ]
    for load in loading:
        load.start()

    barrier = pltpu.get_barrier_semaphore()
    for o in range(1, nt):
        pl.semaphore_signal(barrier, inc=1, device_id={"tensor": z_peer(o)}, device_id_type=MESH)
    for o in range(1, ndp):
        pl.semaphore_signal(barrier, inc=1, device_id={"dp": dp_peer(o)}, device_id_type=MESH)
    pl.semaphore_wait(barrier, nt + ndp - 2)

    def token_copy(b, c, way, s):
        place = stack.at[token_rows(b), pl.ds(c * cw, cw)]
        return copy(
            place, place, act_send.at[way, s], act_recv.at[b, c], tensor=jnp.clip(me + (1 - 2 * way), 0, nt - 1)
        )

    def has_next(way):
        return me < nt - 1 if way == 0 else me > 0

    def origin(way, s):
        b = me - s if way == 0 else me + s
        return b, (b >= 0 if way == 0 else b < nt), jnp.clip(b, 0, nt - 1)

    def weight_copy(q):
        return copy(wall.at[me], wall.at[me], w_send, w_recv.at[me], tensor=q)

    def send_weights(near, where):
        for way in range(2):
            for far in range(nt - 1, 0, -1):
                q = me + far if way == 0 else me - far
                valid = q < nt if way == 0 else q >= 0

                if (far == 1) == near:
                    @pl.when(jnp.logical_and(valid, where))
                    def _():
                        weight_copy(jnp.clip(q, 0, nt - 1)).start()

    at_end = jnp.logical_or(me == 0, me == nt - 1)
    inside = jnp.logical_not(at_end)

    loading[0].wait()
    for o in range(1, nt):
        q = z_peer(o)
        copy(og.at[token_rows(q), :], ogp.at[slot, me], o_send, o_recv, tensor=q).start()
    loading[1].wait()
    for c in range(CHUNKS):
        for way in range(2):
            @pl.when(has_next(way))
            def _():
                token_copy(me, c, way, 0).start()
    for load in loading[2:]:
        load.wait()
    send_weights(True, at_end)

    og_t = og[...].astype(F32).T.astype(BF16)
    left = dot_nt(warm[...], stack[tok:, :])

    inner = jnp.zeros((rank, tok), F32)
    for s in range(1, nt):
        for c in range(CHUNKS):
            for way in range(2):
                _, valid, b = origin(way, s)

                @pl.when(valid)
                def _():
                    token_copy(b, c, way, s).wait_recv()

                @pl.when(jnp.logical_and(valid, has_next(way)))
                def _():
                    token_copy(b, c, way, s).start()
            if s == 1 and c == 0:
                some = pl.ds(0, (nt - 1) * rows)
                copy(og.at[some, :], og.at[some, :], o_send, o_recv, tensor=z_peer(1)).wait_recv()
                for o in range(1, spread):
                    copy(ogp.at[slot], ogp.at[slot], g_send, g_recv, dp=group + group_peer(o)).start()
            if s == nt - 1:
                cols = slice(c * cw, (c + 1) * cw)
                inner += dot_nt(warm[:, cols], stack[:tok, cols])
                if c == CHUNKS // 2:
                    send_weights(False, at_end)

    left += fold3(dot(jnp.concatenate(split3(inner), axis=0), og[...]))
    lefts[dp] = left
    for o in range(1, ndp):
        copy(lefts.at[dp], lefts.at[dp], l_send, l_recv, dp=dp_peer(o)).start()
    send_weights(True, inside)

    for c in range(CHUNKS):
        cols = slice(c * cw, (c + 1) * cw)
        merged[:, cols] = dot(og_t, stack[:tok, cols]) + stack[tok:, cols].astype(F32)

    others = pl.ds(0, ndp - 1)
    copy(lefts.at[others], lefts.at[others], l_send, l_recv, dp=dp_peer(1)).wait_recv()
    send_weights(False, inside)
    total = lefts[0]
    for q in range(1, ndp):
        total += lefts[q]
    left = total * (1.0 / ndp)
    left_split = jnp.concatenate(split3(left), axis=0)
    inner_split = jnp.concatenate(split3(fold3(dot_nt(left_split, og[...]))), axis=0)
    lhs = jnp.concatenate([inner_split, left_split], axis=1)

    core = lax.rem(dp, 2)
    chip = dp // 2
    partner = dp + 1 - 2 * core
    nchip = ndp // 2
    ncol = min(ndp, width // 128)
    nrow = ndp // ncol
    pw, ph = width // ncol, rank // nrow
    subs, sub_rows = parts.shape[0], parts.shape[2]

    def piece(q_chip, q_core, sub=None):
        p = q_core * nchip + q_chip
        r, c = p // ncol, lax.rem(p, ncol)
        start, size = (0, ph) if sub is None else (sub * sub_rows, sub_rows)
        row = pl.ds(pl.multiple_of(r * ph + start, sub_rows), size) if nrow > 1 else pl.ds(start, size)
        return row, pl.ds(pl.multiple_of(c * pw, pw), pw)

    def chip_peer(o):
        return lax.rem(chip + o, nchip)

    def half_copy(i):
        return copy(part.at[piece(i, 1 - core)], halves.at[i], h_send, h_recv.at[i], dp=partner)

    def part_copy(q, sub):
        return copy(part.at[piece(q, core, sub)], parts.at[sub, chip], p_send, p_recv.at[sub], dp=2 * q + core)

    def compute_part(c):
        cols = pl.ds(pl.multiple_of(c * pw, pw), pw)
        part[:, cols] = fold3(dot(lhs, stack[:, cols]))

    if nrow == 1:
        for o in range(nchip):
            i = chip_peer(o + 1)
            compute_part((1 - core) * nchip + i)
            half_copy(i).start()
        for o in range(nchip):
            compute_part(core * nchip + chip_peer(o + 1))
    else:
        for c in range(ncol):
            compute_part(c)
        for o in range(nchip):
            half_copy(chip_peer(o + 1)).start()
    for o in range(1, nchip):
        q = chip_peer(o)
        half_copy(q).wait_recv()
        part[piece(q, core)] += halves[q]
        part_copy(q, 0).start()
    for sub in range(1, subs):
        for o in range(1, nchip):
            part_copy(chip_peer(o), sub).start()

    basis_t, inverse = orthonormal(left)
    basis_out[...] = basis_t
    outer = lax.dot_general(
        basis_t, inverse, (((0,), (0,)), ((), ())), precision=lax.Precision.HIGHEST, preferred_element_type=F32
    )
    high, mid, low = split3(jnp.concatenate([inverse, outer], axis=0))
    final = jnp.concatenate([high, high, mid, high, low, mid], axis=1)

    others = pl.ds(0, spread - 1)
    copy(ogp.at[others], ogp.at[others], g_send, g_recv, dp=partner).wait_recv()
    for o in range(1, nt):
        q = z_peer(o)
        copy(wall.at[q], wall.at[q], w_send, w_recv.at[q], tensor=q).wait_recv()
    grads = jnp.concatenate([ogp[:, b].reshape(spread * rows, head) for b in range(nt)], axis=1)
    igs[...] = dot(grads, wall[...].reshape(nt * head, wc)).astype(BF16).reshape(spread, rows, wc)

    def input_copy(q):
        return copy(igs.at[q], input_grad.at[:, slot_cols(slot)], i_send, i_recv, dp=group + q)

    half_copy(chip).wait_recv()

    def right_copy(q_chip, q_core, sub, target, send, recv):
        place = right.at[piece(q_chip, q_core, sub)]
        return copy(place, place, send, recv.at[sub, q_chip], dp=target)

    for sub in range(subs):
        some = pl.ds(0, nchip - 1)
        copy(parts.at[sub, some], parts.at[sub, some], p_send, p_recv.at[sub], dp=partner).wait_recv()
        mine = part[piece(chip, core, sub)] + halves[chip, sub * sub_rows : (sub + 1) * sub_rows]
        for o in range(1, nchip):
            mine += parts[sub, chip_peer(o)]
        right[piece(chip, core, sub)] = mine * (1.0 / ndp)
        for o in range(1, nchip):
            right_copy(chip, core, sub, 2 * chip_peer(o) + core, r_send, r_recv).start()
        right_copy(chip, core, sub, partner, t_send, t_recv).start()
    for o in range(1, spread):
        input_copy(group_peer(o)).start()
    input_grad[:, slot_cols(slot)] = igs[slot]

    def finish(cols):
        high, mid, low = split3(right[:, cols])
        out = dot(final, jnp.concatenate([high, mid, high, low, high, mid], axis=0))
        factor[:, cols] = out[:rank].astype(BF16)
        residual[:, cols] = (merged[:, cols] - out[rank:]).astype(BF16)

    if nrow == 1:
        finish(piece(chip, core)[1])
        for sub in range(subs):
            right_copy(chip, 1 - core, sub, partner, t_send, t_recv).wait_recv()
        finish(piece(chip, 1 - core)[1])
    for sub in range(subs):
        for o in range(1, nchip):
            q = chip_peer(o)
            right_copy(q, core, sub, partner, r_send, r_recv).wait_recv()
            right_copy(q, core, sub, partner, t_send, t_recv).start()
            if nrow == 1 and sub == subs - 1:
                finish(piece(q, core)[1])
    for o in range(1 if nrow == 1 else 0, nchip):
        q = chip_peer(o)
        for sub in range(subs):
            right_copy(q, 1 - core, sub, partner, t_send, t_recv).wait_recv()
        if nrow == 1:
            finish(piece(q, 1 - core)[1])
    if nrow > 1:
        for c in range(ncol):
            finish(pl.ds(c * pw, pw))

    others = pl.ds(0, spread - 1)
    copy(igs.at[others], igs.at[others], i_send, i_recv, dp=partner).wait_recv()

    for way in range(2):
        for s in range(nt):
            _, valid, b = origin(way, s)

            @pl.when(jnp.logical_and(valid, has_next(way)))
            def _():
                place = stack.at[token_rows(b), :]
                copy(place, place, act_send.at[way, s], act_recv.at[b, 0], tensor=z_peer(1)).wait_send()

    def sent(ref, send, recv):
        copy(ref, ref, send, recv, dp=partner).wait_send()

    sent(og.at[pl.ds(0, (nt - 1) * rows), :], o_send, o_recv)
    sent(ogp.at[others], g_send, g_recv)
    sent(wall.at[pl.ds(0, nt - 1)], w_send, w_recv.at[0])
    sent(igs.at[others], i_send, i_recv)
    sent(lefts.at[pl.ds(0, ndp - 1)], l_send, l_recv)
    sent(halves, h_send, h_recv.at[0])
    some = parts.at[:, pl.ds(0, nchip - 1)]
    sent(some, p_send, p_recv.at[0])
    sent(some, r_send, r_recv.at[0, 0])
    sent(halves, t_send, t_recv.at[0, 0])


def write_out(*refs):
    sems = refs[8]
    copies = []
    for i in range(4):
        src, dst = refs[i], refs[4 + i]
        count = PIECES if i == 0 else 2
        step = src.shape[0] // count
        for j in range(count):
            rows = pl.ds(j * step, step)
            copies.append(pltpu.make_async_copy(src.at[rows], dst.at[rows], sems.at[i, j]))
    for c in copies:
        c.start()
    for c in copies:
        c.wait()


def local(activations, out_grad, value_weight, error_feedback, warm_right):
    ndp, nt = lax.axis_size("dp"), lax.axis_size("tensor")
    layers = [[], [], [], []]
    for layer in range(activations.shape[0]):
        outs = one_layer(
            ndp, nt, activations[layer], out_grad[layer], value_weight[layer],
            error_feedback[layer, 0], warm_right[layer, 0].T,
        )
        for kept, out in zip(layers, outs):
            kept.append(out)
    residual, basis, factor, input_grad = [jnp.stack(kept) for kept in layers]
    return residual[:, None], basis.swapaxes(1, 2), factor.swapaxes(1, 2)[:, None], input_grad


def one_layer(ndp, nt, act, og, weight, error, warm):
    rows, width = act.shape
    tok, head = og.shape
    rank = warm.shape[0]
    spread = min(ndp, 8)
    ncol = min(ndp, width // 128)
    nrow = ndp // ncol
    nchip = ndp // 2
    ph, pw = rank // nrow, width // ncol
    subs = min(SUBS, ph // 8)
    dma = pltpu.SemaphoreType.DMA
    vmem = pl.BlockSpec(memory_space=pltpu.VMEM)
    shapes = (((head, width), BF16), ((rank, head), F32), ((rank, width), BF16), ((rows, width), BF16))
    results = pl.pallas_call(
        functools.partial(kernel, ndp, nt),
        out_shape=tuple(pltpu.VMEM(shape, dtype) for shape, dtype in shapes),
        in_specs=[pl.BlockSpec(memory_space=pltpu.HBM)] * 5,
        out_specs=(vmem,) * 4,
        scratch_shapes=[
            pltpu.VMEM((tok, head), BF16),
            pltpu.VMEM((tok + head, width), BF16),
            pltpu.VMEM((rank, width), BF16),
            pltpu.VMEM((nt, head, width // spread), BF16),
            pltpu.VMEM((spread, nt, rows, head), BF16),
            pltpu.VMEM((spread, rows, width // spread), BF16),
            pltpu.VMEM((head, width), F32),
            pltpu.VMEM((ndp, rank, head), F32),
            pltpu.VMEM((rank, width), F32),
            pltpu.VMEM((nchip, ph, pw), F32),
            pltpu.VMEM((subs, nchip, ph // subs, pw), F32),
            pltpu.VMEM((rank, width), F32),
            dma((6,)),
            dma((2, nt)), dma((nt, CHUNKS)),
            dma, dma, dma, dma,
            dma, dma((nt,)),
            dma, dma,
            dma, dma,
            dma, dma((nchip,)),
            dma, dma((subs,)),
            dma, dma((subs, nchip)),
            dma, dma((subs, nchip)),
        ],
        compiler_params=pltpu.CompilerParams(
            collective_id=0, has_side_effects=True, vmem_limit_bytes=62 * 1024 * 1024
        ),
    )(act, og, weight, error, warm)
    return pl.pallas_call(
        write_out,
        out_shape=tuple(jax.ShapeDtypeStruct(shape, dtype) for shape, dtype in shapes),
        in_specs=[vmem] * 4,
        out_specs=(pl.BlockSpec(memory_space=pltpu.HBM),) * 4,
        scratch_shapes=[dma((4, PIECES))],
        compiler_params=pltpu.CompilerParams(vmem_limit_bytes=16 * 1024 * 1024),
    )(*results)


def solution(mesh):
    return jax.shard_map(
        local,
        mesh=mesh,
        in_specs=(
            P(None, ("dp", "tensor"), None),
            P(None, "dp", "tensor"),
            P(None, "tensor", None),
            P(None, "dp", "tensor", None),
            P(None, "tensor", None, None),
        ),
        out_specs=(
            P(None, "dp", "tensor", None),
            P(None, "tensor", None),
            P(None, "tensor", None, None),
            P(None, ("dp", "tensor"), None),
        ),
        check_vma=False,
    )
```

time: 56.4 us -> 48.4 us (0.86)
  Pallas kernels: 55.6 us -> 47.6 us
    pallas_call x1, Pallas kernels: 54.3 us -> 46.3 us  [one_layer(): pl.pallas_call(functools.partial(kernel, ndp, nt), out_shape=tuple((pltpu...]
where the time goes in v2:
time: 48.4 us; the launch traced here: 48.2 us
  Pallas kernels  47.6 us (98%)
  between operations  0.64 us (1%)
    pallas_call x1, Pallas kernels, one_layer(): pl.pallas_call(functools.partial(kernel, ndp, nt), out_shape=tuple((pltpu...  46.3 us
    pallas_call x1, Pallas kernels, one_layer(): pl.pallas_call(write_out, out_shape=tuple((jax.ShapeDtypeStruct(shape, dt...  1.28 us

profile of v2, /device:TPU:0, one launch (start us, length us, event | category | flops | bytes accessed | tf_op | source)
XLA Modules:
  0.0 48.2 jit_solution(3545086076855818141)
XLA Ops:
  0.6 46.3 %shard_map.84 = (bf16[128,4096]{1,0:T(8,128)(2,1)S(1)}, f32[32,128]{1,0:T(8,128)S(1)}, bf16[32,4096]{1,0:T(8,128)(2,1)S(1)}, bf16[32,4096]{1,0:T(8,128)(2,1)S(1)}) custom-call(bf16[32,4096]{1,0:T(8,128)(2,1)} %bitcast.19, bf16[128,128]{1,0:T(8,128)(2,1)} %bitcast.21, bf16[128,4096]{1,0:T(8,128)(2,1)} %bitcast.17, bf16[128,4096]{1,0:T(8,128)(2,1)} %bitcast.18, ...), custom_call_target="tpu_custom_call" | custom-call | tf_op jit(solution)/shard_map/pallas_call | solution.py:390
  46.9 1.3 %shard_map.85 = (bf16[128,4096]{1,0:T(8,128)(2,1)}, f32[32,128]{1,0:T(8,128)}, bf16[32,4096]{1,0:T(8,128)(2,1)}, bf16[32,4096]{1,0:T(8,128)(2,1)}) custom-call(bf16[128,4096]{1,0:T(8,128)(2,1)S(1)} %get-tuple-element.12.refs_0_, f32[32,128]{1,0:T(8,128)S(1)} %get-tuple-element.13.refs_1_, bf16[32,4096]{1,0:T(8,128)(2,1)S(1)} %get-tuple-element.14.refs_2_, ...), custom_call_target="tpu_custom_call" | custom-call | tf_op jit(solution)/shard_map/pallas_call | solution.py:423

commit v3 on v2

--- a/solution.py
+++ b/solution.py
@@ -13,6 +13,7 @@
 CHUNKS = 4
 PIECES = 4
 SUBS = 2
+HELD = 2
 
 
 def split3(x):
@@ -56,15 +57,15 @@
 def kernel(
     ndp, nt, act_hbm, og_hbm, weight_hbm, error_hbm, warm_hbm,
     residual, basis_out, factor, input_grad,
-    og, stack, warm, wall, ogp, igs, merged, lefts, part, halves, parts, right,
-    loads, act_send, act_recv, o_send, o_recv, g_send, g_recv, w_send, w_recv, i_send, i_recv,
+    og, stack, warm, inner, told, wall, ogp, igs, merged, lefts, part, halves, parts, right,
+    loads, act_send, act_recv, f_send, f_recv, n_send, n_recv, o_send, o_recv, g_send, g_recv, w_send, w_recv, i_send, i_recv,
     l_send, l_recv, h_send, h_recv, p_send, p_recv, r_send, r_recv, t_send, t_recv,
 ):
     dp = lax.axis_index("dp")
     me = lax.axis_index("tensor")
     rows, width = act_hbm.shape
     tok, head = og.shape
-    rank = warm.shape[0]
+    rank = told.shape[0]
     spread = ogp.shape[0]
     cw = width // CHUNKS
     wc = width // spread
@@ -95,7 +96,7 @@
         pltpu.make_async_copy(src, dst, loads.at[i])
         for i, (src, dst) in enumerate((
             (og_hbm, og), (act_hbm, stack.at[token_rows(me), :]), (og_hbm.at[token_rows(me), :], ogp.at[slot, me]),
-            (warm_hbm, warm), (error_hbm, stack.at[pl.ds(tok, head), :]), (weight_hbm.at[:, slot_cols(slot)], wall.at[me]),
+            (warm_hbm, warm.at[pl.ds(0, rank), :]), (error_hbm, stack.at[pl.ds(tok, head), :]), (weight_hbm.at[:, slot_cols(slot)], wall.at[me]),
         ))
     ]
     for load in loading:
@@ -131,12 +132,30 @@
                 valid = q < nt if way == 0 else q >= 0
 
                 if (far == 1) == near:
-                    @pl.when(jnp.logical_and(valid, where))
+                    @pl.when(valid if where is True else jnp.logical_and(valid, where))
                     def _():
                         weight_copy(jnp.clip(q, 0, nt - 1)).start()
 
     at_end = jnp.logical_or(me == 0, me == nt - 1)
     inside = jnp.logical_not(at_end)
+    core = lax.rem(dp, 2)
+    partner = dp + 1 - 2 * core
+    helped = nt == 4
+    neighbour = jnp.where(me == 0, 1, jnp.where(me == nt - 1, nt - 2, jnp.where(me == 1, 0, nt - 1)))
+
+    def warm_half(which):
+        return pl.ds(pl.multiple_of(which * (width // 2), width // 2), width // 2)
+
+    def warm_copy(**device):
+        src = warm.at[pl.ds(0, rank), warm_half(core)]
+        return copy(src, warm.at[pl.ds(rank, rank), warm_half(core)], f_send, f_recv.at[0], **device)
+
+    def warm_share(which):
+        place = warm.at[pl.ds(rank, rank), warm_half(which)]
+        return copy(place, place, f_send, f_recv.at[1], dp=partner)
+
+    def told_copy():
+        return copy(inner.at[pl.ds(rank, rank), :], told, n_send, n_recv, tensor=neighbour)
 
     loading[0].wait()
     for o in range(1, nt):
@@ -150,13 +169,22 @@
                 token_copy(me, c, way, 0).start()
     for load in loading[2:]:
         load.wait()
+    if helped:
+        @pl.when(at_end)
+        def _():
+            warm_copy(tensor=neighbour).start()
     send_weights(True, at_end)
 
     og_t = og[...].astype(F32).T.astype(BF16)
-    left = dot_nt(warm[...], stack[tok:, :])
-
-    inner = jnp.zeros((rank, tok), F32)
+    left_error = dot_nt(warm[:rank, :], stack[tok:, :])
+
+    def send_left(product):
+        lefts[dp] = left_error + fold3(dot(jnp.concatenate(split3(product), axis=0), og[...]))
+        for o in range(1, ndp):
+            copy(lefts.at[dp], lefts.at[dp], l_send, l_recv, dp=dp_peer(o)).start()
+
     for s in range(1, nt):
+        help_now = helped and s == nt - 2
         for c in range(CHUNKS):
             for way in range(2):
                 _, valid, b = origin(way, s)
@@ -165,25 +193,53 @@
                 def _():
                     token_copy(b, c, way, s).wait_recv()
 
-                @pl.when(jnp.logical_and(valid, has_next(way)))
-                def _():
-                    token_copy(b, c, way, s).start()
+                if not (help_now and c >= HELD):
+                    @pl.when(jnp.logical_and(valid, has_next(way)))
+                    def _():
+                        token_copy(b, c, way, s).start()
             if s == 1 and c == 0:
                 some = pl.ds(0, (nt - 1) * rows)
                 copy(og.at[some, :], og.at[some, :], o_send, o_recv, tensor=z_peer(1)).wait_recv()
                 for o in range(1, spread):
                     copy(ogp.at[slot], ogp.at[slot], g_send, g_recv, dp=group + group_peer(o)).start()
-            if s == nt - 1:
-                cols = slice(c * cw, (c + 1) * cw)
-                inner += dot_nt(warm[:, cols], stack[:tok, cols])
-                if c == CHUNKS // 2:
-                    send_weights(False, at_end)
-
-    left += fold3(dot(jnp.concatenate(split3(inner), axis=0), og[...]))
-    lefts[dp] = left
-    for o in range(1, ndp):
-        copy(lefts.at[dp], lefts.at[dp], l_send, l_recv, dp=dp_peer(o)).start()
-    send_weights(True, inside)
+            if help_now and c == HELD - 1:
+                @pl.when(inside)
+                def _():
+                    warm_copy(tensor=neighbour).wait_recv()
+                    warm_share(core).start()
+            if help_now and c == CHUNKS - 2:
+                @pl.when(inside)
+                def _():
+                    warm_share(1 - core).wait_recv()
+                    inner[...] = dot_nt(warm[:, : (c + 1) * cw], stack[:tok, : (c + 1) * cw])
+            if s == nt - 1 and c == CHUNKS // 2 - 1 and helped:
+                @pl.when(at_end)
+                def _():
+                    told_copy().wait_recv()
+                    send_left(told[...])
+            if s == nt - 1 and c == CHUNKS // 2:
+                send_weights(False, at_end)
+        if help_now:
+            @pl.when(inside)
+            def _():
+                last = slice((CHUNKS - 1) * cw, width)
+                inner[...] += dot_nt(warm[:, last], stack[:tok, last])
+                told_copy().start()
+            for c in range(HELD, CHUNKS):
+                for way in range(2):
+                    _, valid, b = origin(way, s)
+
+                    @pl.when(jnp.logical_and(valid, has_next(way)))
+                    def _():
+                        token_copy(b, c, way, s).start()
+
+            @pl.when(inside)
+            def _():
+                send_left(inner[:rank, :])
+                send_weights(True, True)
+    if not helped:
+        send_left(dot_nt(warm[:rank, :], stack[:tok, :]))
+        send_weights(True, inside)
 
     for c in range(CHUNKS):
         cols = slice(c * cw, (c + 1) * cw)
@@ -200,9 +256,7 @@
     inner_split = jnp.concatenate(split3(fold3(dot_nt(left_split, og[...]))), axis=0)
     lhs = jnp.concatenate([inner_split, left_split], axis=1)
 
-    core = lax.rem(dp, 2)
     chip = dp // 2
-    partner = dp + 1 - 2 * core
     nchip = ndp // 2
     ncol = min(ndp, width // 128)
     nrow = ndp // ncol
@@ -258,17 +312,6 @@
     high, mid, low = split3(jnp.concatenate([inverse, outer], axis=0))
     final = jnp.concatenate([high, high, mid, high, low, mid], axis=1)
 
-    others = pl.ds(0, spread - 1)
-    copy(ogp.at[others], ogp.at[others], g_send, g_recv, dp=partner).wait_recv()
-    for o in range(1, nt):
-        q = z_peer(o)
-        copy(wall.at[q], wall.at[q], w_send, w_recv.at[q], tensor=q).wait_recv()
-    grads = jnp.concatenate([ogp[:, b].reshape(spread * rows, head) for b in range(nt)], axis=1)
-    igs[...] = dot(grads, wall[...].reshape(nt * head, wc)).astype(BF16).reshape(spread, rows, wc)
-
-    def input_copy(q):
-        return copy(igs.at[q], input_grad.at[:, slot_cols(slot)], i_send, i_recv, dp=group + q)
-
     half_copy(chip).wait_recv()
 
     def right_copy(q_chip, q_core, sub, target, send, recv):
@@ -285,6 +328,17 @@
         for o in range(1, nchip):
             right_copy(chip, core, sub, 2 * chip_peer(o) + core, r_send, r_recv).start()
         right_copy(chip, core, sub, partner, t_send, t_recv).start()
+    others = pl.ds(0, spread - 1)
+    copy(ogp.at[others], ogp.at[others], g_send, g_recv, dp=partner).wait_recv()
+    for o in range(1, nt):
+        q = z_peer(o)
+        copy(wall.at[q], wall.at[q], w_send, w_recv.at[q], tensor=q).wait_recv()
+    grads = jnp.concatenate([ogp[:, b].reshape(spread * rows, head) for b in range(nt)], axis=1)
+    igs[...] = dot(grads, wall[...].reshape(nt * head, wc)).astype(BF16).reshape(spread, rows, wc)
+
+    def input_copy(q):
+        return copy(igs.at[q], input_grad.at[:, slot_cols(slot)], i_send, i_recv, dp=group + q)
+
     for o in range(1, spread):
         input_copy(group_peer(o)).start()
     input_grad[:, slot_cols(slot)] = igs[slot]
@@ -332,6 +386,16 @@
     def sent(ref, send, recv):
         copy(ref, ref, send, recv, dp=partner).wait_send()
 
+    if helped:
+        @pl.when(at_end)
+        def _():
+            copy(warm.at[pl.ds(0, rank), warm_half(0)], warm.at[pl.ds(0, rank), warm_half(0)], f_send, f_recv.at[0], dp=partner).wait_send()
+
+        @pl.when(inside)
+        def _():
+            warm_share(core).wait_send()
+            told_copy().wait_send()
+
     sent(og.at[pl.ds(0, (nt - 1) * rows), :], o_send, o_recv)
     sent(ogp.at[others], g_send, g_recv)
     sent(wall.at[pl.ds(0, nt - 1)], w_send, w_recv.at[0])
@@ -395,7 +459,9 @@
         scratch_shapes=[
             pltpu.VMEM((tok, head), BF16),
             pltpu.VMEM((tok + head, width), BF16),
-            pltpu.VMEM((rank, width), BF16),
+            pltpu.VMEM((2 * rank, width), BF16),
+            pltpu.VMEM((2 * rank, tok), F32),
+            pltpu.VMEM((rank, tok), F32),
             pltpu.VMEM((nt, head, width // spread), BF16),
             pltpu.VMEM((spread, nt, rows, head), BF16),
             pltpu.VMEM((spread, rows, width // spread), BF16),
@@ -407,6 +473,7 @@
             pltpu.VMEM((rank, width), F32),
             dma((6,)),
             dma((2, nt)), dma((nt, CHUNKS)),
+            dma, dma((2,)), dma, dma,
             dma, dma, dma, dma,
             dma, dma((nt,)),
             dma, dma,

time: 48.4 us -> 43.1 us (0.89)
  Pallas kernels: 47.6 us -> 42.3 us
    pallas_call x1, Pallas kernels: 46.3 us -> 41 us  [one_layer(): pl.pallas_call(functools.partial(kernel, ndp, nt), out_shape=tuple((pltpu...]
where the time goes in v3:
time: 43.1 us; the launch traced here: 43 us
  Pallas kernels  42.3 us (98%)
  between operations  0.64 us (1%)
    pallas_call x1, Pallas kernels, one_layer(): pl.pallas_call(functools.partial(kernel, ndp, nt), out_shape=tuple((pltpu...  41 us
    pallas_call x1, Pallas kernels, one_layer(): pl.pallas_call(write_out, out_shape=tuple((jax.ShapeDtypeStruct(shape, dt...  1.28 us

profile of v3, /device:TPU:0, one launch (start us, length us, event | category | flops | bytes accessed | tf_op | source)
XLA Modules:
  0.0 43.0 jit_solution(5277788418562233264)
XLA Ops:
  0.6 41.0 %shard_map.84 = (bf16[128,4096]{1,0:T(8,128)(2,1)S(1)}, f32[32,128]{1,0:T(8,128)S(1)}, bf16[32,4096]{1,0:T(8,128)(2,1)S(1)}, bf16[32,4096]{1,0:T(8,128)(2,1)S(1)}) custom-call(bf16[32,4096]{1,0:T(8,128)(2,1)} %bitcast.19, bf16[128,128]{1,0:T(8,128)(2,1)} %bitcast.21, bf16[128,4096]{1,0:T(8,128)(2,1)} %bitcast.17, bf16[128,4096]{1,0:T(8,128)(2,1)} %bitcast.18, ...), custom_call_target="tpu_custom_call" | custom-call | tf_op jit(solution)/shard_map/pallas_call | solution.py:454
  41.7 1.3 %shard_map.85 = (bf16[128,4096]{1,0:T(8,128)(2,1)}, f32[32,128]{1,0:T(8,128)}, bf16[32,4096]{1,0:T(8,128)(2,1)}, bf16[32,4096]{1,0:T(8,128)(2,1)}) custom-call(bf16[128,4096]{1,0:T(8,128)(2,1)S(1)} %get-tuple-element.12.refs_0_, f32[32,128]{1,0:T(8,128)S(1)} %get-tuple-element.13.refs_1_, bf16[32,4096]{1,0:T(8,128)(2,1)S(1)} %get-tuple-element.14.refs_2_, ...), custom_call_target="tpu_custom_call" | custom-call | tf_op jit(solution)/shard_map/pallas_call | solution.py:490

commit v4 on v3

--- a/solution.py
+++ b/solution.py
@@ -12,7 +12,7 @@
 BF16 = jnp.bfloat16
 CHUNKS = 4
 PIECES = 4
-SUBS = 2
+SUBS = 4
 HELD = 2
 
 
@@ -77,6 +77,12 @@
             src_ref=src, dst_ref=dst, send_sem=send, recv_sem=recv, device_id=device, device_id_type=MESH
         )
 
+    def issue(*copies):
+        @pl.when(dp >= 0)
+        def _():
+            for c in copies:
+                c.start()
+
     def z_peer(o):
         return lax.rem(me + o, nt)
 
@@ -158,9 +164,9 @@
         return copy(inner.at[pl.ds(rank, rank), :], told, n_send, n_recv, tensor=neighbour)
 
     loading[0].wait()
-    for o in range(1, nt):
-        q = z_peer(o)
-        copy(og.at[token_rows(q), :], ogp.at[slot, me], o_send, o_recv, tensor=q).start()
+    issue(*(
+        copy(og.at[token_rows(z_peer(o)), :], ogp.at[slot, me], o_send, o_recv, tensor=z_peer(o)) for o in range(1, nt)
+    ))
     loading[1].wait()
     for c in range(CHUNKS):
         for way in range(2):
@@ -180,8 +186,7 @@
 
     def send_left(product):
         lefts[dp] = left_error + fold3(dot(jnp.concatenate(split3(product), axis=0), og[...]))
-        for o in range(1, ndp):
-            copy(lefts.at[dp], lefts.at[dp], l_send, l_recv, dp=dp_peer(o)).start()
+        issue(*(copy(lefts.at[dp], lefts.at[dp], l_send, l_recv, dp=dp_peer(o)) for o in range(1, ndp)))
 
     for s in range(1, nt):
         help_now = helped and s == nt - 2
@@ -200,8 +205,9 @@
             if s == 1 and c == 0:
                 some = pl.ds(0, (nt - 1) * rows)
                 copy(og.at[some, :], og.at[some, :], o_send, o_recv, tensor=z_peer(1)).wait_recv()
-                for o in range(1, spread):
-                    copy(ogp.at[slot], ogp.at[slot], g_send, g_recv, dp=group + group_peer(o)).start()
+                issue(*(
+                    copy(ogp.at[slot], ogp.at[slot], g_send, g_recv, dp=group + group_peer(o)) for o in range(1, spread)
+                ))
             if help_now and c == HELD - 1:
                 @pl.when(inside)
                 def _():
@@ -287,22 +293,19 @@
         for o in range(nchip):
             i = chip_peer(o + 1)
             compute_part((1 - core) * nchip + i)
-            half_copy(i).start()
+            issue(half_copy(i))
         for o in range(nchip):
             compute_part(core * nchip + chip_peer(o + 1))
     else:
         for c in range(ncol):
             compute_part(c)
-        for o in range(nchip):
-            half_copy(chip_peer(o + 1)).start()
+        issue(*(half_copy(chip_peer(o + 1)) for o in range(nchip)))
     for o in range(1, nchip):
         q = chip_peer(o)
         half_copy(q).wait_recv()
         part[piece(q, core)] += halves[q]
-        part_copy(q, 0).start()
-    for sub in range(1, subs):
-        for o in range(1, nchip):
-            part_copy(chip_peer(o), sub).start()
+        issue(part_copy(q, 0))
+    issue(*(part_copy(chip_peer(o), sub) for sub in range(1, subs) for o in range(1, nchip)))
 
     basis_t, inverse = orthonormal(left)
     basis_out[...] = basis_t
@@ -325,9 +328,10 @@
         for o in range(1, nchip):
             mine += parts[sub, chip_peer(o)]
         right[piece(chip, core, sub)] = mine * (1.0 / ndp)
-        for o in range(1, nchip):
-            right_copy(chip, core, sub, 2 * chip_peer(o) + core, r_send, r_recv).start()
-        right_copy(chip, core, sub, partner, t_send, t_recv).start()
+        issue(
+            *(right_copy(chip, core, sub, 2 * chip_peer(o) + core, r_send, r_recv) for o in range(1, nchip)),
+            right_copy(chip, core, sub, partner, t_send, t_recv),
+        )
     others = pl.ds(0, spread - 1)
     copy(ogp.at[others], ogp.at[others], g_send, g_recv, dp=partner).wait_recv()
     for o in range(1, nt):
@@ -339,8 +343,7 @@
     def input_copy(q):
         return copy(igs.at[q], input_grad.at[:, slot_cols(slot)], i_send, i_recv, dp=group + q)
 
-    for o in range(1, spread):
-        input_copy(group_peer(o)).start()
+    issue(*(input_copy(group_peer(o)) for o in range(1, spread)))
     input_grad[:, slot_cols(slot)] = igs[slot]
 
     def finish(cols):
@@ -358,7 +361,7 @@
         for o in range(1, nchip):
             q = chip_peer(o)
             right_copy(q, core, sub, partner, r_send, r_recv).wait_recv()
-            right_copy(q, core, sub, partner, t_send, t_recv).start()
+            issue(right_copy(q, core, sub, partner, t_send, t_recv))
             if nrow == 1 and sub == subs - 1:
                 finish(piece(q, core)[1])
     for o in range(1 if nrow == 1 else 0, nchip):

time: 43.1 us -> 40.8 us (0.947)
  Pallas kernels: 42.3 us -> 40.1 us
    pallas_call x1, Pallas kernels: 41 us -> 38.8 us  [one_layer(): pl.pallas_call(functools.partial(kernel, ndp, nt), out_shape=tuple((pltpu...]
where the time goes in v4:
time: 40.8 us; the launch traced here: 40.7 us
  Pallas kernels  40.1 us (98%)
  between operations  0.64 us (2%)
    pallas_call x1, Pallas kernels, one_layer(): pl.pallas_call(functools.partial(kernel, ndp, nt), out_shape=tuple((pltpu...  38.8 us
    pallas_call x1, Pallas kernels, one_layer(): pl.pallas_call(write_out, out_shape=tuple((jax.ShapeDtypeStruct(shape, dt...  1.28 us

profile of v4, /device:TPU:0, one launch (start us, length us, event | category | flops | bytes accessed | tf_op | source)
XLA Modules:
  0.0 40.7 jit_solution(5221883537786707960)
XLA Ops:
  0.6 38.8 %shard_map.84 = (bf16[128,4096]{1,0:T(8,128)(2,1)S(1)}, f32[32,128]{1,0:T(8,128)S(1)}, bf16[32,4096]{1,0:T(8,128)(2,1)S(1)}, bf16[32,4096]{1,0:T(8,128)(2,1)S(1)}) custom-call(bf16[32,4096]{1,0:T(8,128)(2,1)} %bitcast.19, bf16[128,128]{1,0:T(8,128)(2,1)} %bitcast.21, bf16[128,4096]{1,0:T(8,128)(2,1)} %bitcast.17, bf16[128,4096]{1,0:T(8,128)(2,1)} %bitcast.18, ...), custom_call_target="tpu_custom_call" | custom-call | tf_op jit(solution)/shard_map/pallas_call | solution.py:457
  39.4 1.3 %shard_map.85 = (bf16[128,4096]{1,0:T(8,128)(2,1)}, f32[32,128]{1,0:T(8,128)}, bf16[32,4096]{1,0:T(8,128)(2,1)}, bf16[32,4096]{1,0:T(8,128)(2,1)}) custom-call(bf16[128,4096]{1,0:T(8,128)(2,1)S(1)} %get-tuple-element.12.refs_0_, f32[32,128]{1,0:T(8,128)S(1)} %get-tuple-element.13.refs_1_, bf16[32,4096]{1,0:T(8,128)(2,1)S(1)} %get-tuple-element.14.refs_2_, ...), custom_call_target="tpu_custom_call" | custom-call | tf_op jit(solution)/shard_map/pallas_call | solution.py:493
